TPU v7x, 32 devices: a whole 2x2x4 slice. The times are simulated.
32 devices in a mesh: sub: 16 (over z, y, x), crs: 2 (over core).
Axes of the slice: x: 2, y: 2, z: 4, core: 2. Of those that a mesh axis runs over, the one named last changes fastest.
Arguments:
- multipliers: float32 [16, 128, 512], P(None, ('sub', 'crs')), may hold values from -6 to 6
- own_modes: float32 [6, 128, 512], P(None, ('sub', 'crs')), may hold values from -0.75 to 0.75
- neighbour_modes: float32 [6, 128, 512], P(None, ('sub', 'crs')), may hold values from -0.75 to 0.75
- face_index: int32 [128, 512], P(('sub', 'crs')), may hold values from 0 to 5, as said below
- neighbour_list: int32 [128, 6], replicated, may hold values from 0 to 127, as said below
- coarse_factor: float32 [768, 768], P('sub', 'crs'), may hold values from -0.21875 to 0.21875
Outputs:
- projected: float32 [16, 128, 512], P(None, ('sub', 'crs'))
Inputs may be any that keep to these rules, and one draw needn't show every extreme that they name: `face_index`: the multipliers of each subdomain lie in 6 contiguous nonempty blocks, face 0 first and face 5 last. `neighbour_list`: subdomain s = (8 x + y) * 8 + z sits at (x, y, z) of a periodic grid of 2 x 8 x 8 subdomains; the 6 faces of each subdomain name its grid neighbours x plus 1, x minus 1, y plus or minus 1, z plus or minus 1 (periodic; along the first dimension both name the same subdomain), in an order that differs from subdomain to subdomain.
All inputs are finite; a program needn't handle non-finite values.
Results may differ from a plain program's by a relative error of at most 0.0001.
Values sent between devices are 32-bit elements; how exact they have to be, the bound alone decides.
A program may use at most 64 MiB of HBM per device.

v0:
```python
import jax
import jax.numpy as jnp
from jax import lax
from jax.sharding import PartitionSpec as P

MODES = 6
NFACE = 6
HIGHEST = lax.Precision.HIGHEST


def shifted(value, axis, by):
    peers = lax.axis_size(axis)
    return lax.ppermute(value, axis, [(i, (i + by) % peers) for i in range(peers)])


def select_columns(portion, positions, wanted):
    matches = (positions[:, None] == wanted[None, :]).astype(jnp.float32)
    return jnp.einsum("krn,nt->krt", portion, matches, precision=HIGHEST)


def body(multipliers, own_modes, neighbour_modes, face_index, neighbour_list, coarse_factor):
    width_rhs = multipliers.shape[0]
    local_subs = multipliers.shape[1]
    crs_size = lax.axis_size("crs")
    sub_size = lax.axis_size("sub")
    crs_rank = lax.axis_index("crs")
    sub_rank = lax.axis_index("sub")
    group_subs = local_subs * crs_size
    faces_dev = local_subs * NFACE
    first_sub = (sub_rank * crs_size + crs_rank) * local_subs
    flat_targets = neighbour_list.reshape(-1)
    row_len = sub_size // 2
    col_len = sub_size // row_len
    row_place = sub_rank % row_len
    local_ids = first_sub + lax.iota(jnp.int32, local_subs)
    first = local_ids // (row_len * group_subs)
    second = local_ids // group_subs % row_len
    third = local_ids % group_subs

    def place(a, b, c):
        return (a * row_len + b) * group_subs + c

    grid_next = jnp.stack(
        [
            place((first + 1) % col_len, second, third),
            place((first + col_len - 1) % col_len, second, third),
            place(first, (second + 1) % row_len, third),
            place(first, (second + row_len - 1) % row_len, third),
            place(first, second, (third + 1) % group_subs),
            place(first, second, (third + group_subs - 1) % group_subs),
        ],
        axis=1,
    )
    local_nbrs = lax.dynamic_slice_in_dim(neighbour_list, first_sub, local_subs, 0)
    matches = (local_nbrs[:, :, None] == grid_next[:, None, :]).astype(jnp.int32)
    first_hit = matches * (jnp.cumsum(matches, axis=2) == 1).astype(jnp.int32)
    face_dir = first_hit.astype(jnp.float32)
    masked_modes = []
    for which_face in range(NFACE):
        masked_modes.append(neighbour_modes * (face_index == which_face).astype(jnp.float32)[None])
    own_coarse = jnp.einsum("ksm,rsm->krs", own_modes, multipliers, precision=HIGHEST)
    face_parts = []
    for which_face in range(NFACE):
        face_parts.append(
            jnp.einsum("ksm,rsm->krs", masked_modes[which_face], multipliers, precision=HIGHEST)
        )
    face_stack = jnp.stack(face_parts, axis=3)
    outgoing = jnp.einsum("krjf,jfd->dkrj", face_stack, face_dir, precision=HIGHEST)
    plans = [(0, row_len), (1, -row_len), (2, 1), (2, 1 - row_len), (3, -1), (3, row_len - 1)]
    arrived = []
    for direction, step in plans:
        arrived.append(shifted(outgoing[direction], "sub", step))
    plus_y = jnp.where(row_place == 0, arrived[3], arrived[2])
    minus_y = jnp.where(row_place == row_len - 1, arrived[5], arrived[4])
    upward = outgoing[4]
    downward = outgoing[5]
    crossing = []
    for piece, step in ((upward[:, :, -1:], 1), (downward[:, :, :1], -1)):
        crossing.append(shifted(piece, "crs", step))
    from_below = jnp.concatenate([crossing[0], upward[:, :, :-1]], axis=2)
    from_above = jnp.concatenate([downward[:, :, 1:], crossing[1]], axis=2)
    own_total = own_coarse + arrived[0] + arrived[1] + plus_y + minus_y + from_below + from_above
    group_coarse = lax.all_gather(own_total, "crs", axis=2, tiled=True)
    coarse_rhs = group_coarse.transpose(2, 0, 1).reshape(group_subs * MODES, width_rhs)
    partial_rows = jnp.einsum("cp,cr->pr", coarse_factor, coarse_rhs, precision=HIGHEST)
    panel_rows = lax.psum(partial_rows, "sub")
    partial_modes = jnp.dot(
        coarse_factor, panel_rows, precision=HIGHEST, preferred_element_type=jnp.float32
    )
    partial_modes = partial_modes.reshape(group_subs, MODES, width_rhs).transpose(1, 2, 0)
    local_targets = lax.dynamic_slice_in_dim(flat_targets, first_sub * NFACE, faces_dev)
    group_amps = lax.psum(partial_modes, "crs")
    own_amps = lax.dynamic_slice_in_dim(group_amps, crs_rank * local_subs, local_subs, 2)
    portion = lax.all_gather(group_amps, "sub", axis=2, tiled=True)
    positions = lax.iota(jnp.int32, portion.shape[2])
    near_amps = select_columns(portion, positions, local_targets)
    near_amps = near_amps.reshape(MODES, width_rhs, local_subs, NFACE)
    applied = jnp.einsum("ksm,krs->rsm", own_modes, own_amps, precision=HIGHEST)
    for which_face in range(NFACE):
        applied = applied + jnp.einsum(
            "ksm,krs->rsm",
            masked_modes[which_face],
            near_amps[:, :, :, which_face],
            precision=HIGHEST,
        )
    return multipliers - applied


def solution(mesh):
    placed = (
        P(None, ("sub", "crs"), None),
        P(None, ("sub", "crs"), None),
        P(None, ("sub", "crs"), None),
        P(("sub", "crs"), None),
        P(),
        P("sub", "crs"),
    )
    return jax.shard_map(
        body, mesh=mesh, in_specs=placed, out_specs=P(None, ("sub", "crs"), None), check_vma=False
    )
```

profile of v0, /device:TPU:0, one launch (start us, length us, event | category | flops | bytes accessed | tf_op | source)
XLA Modules:
  0.0 146.9 jit_solution(12411067293623808287)
XLA Ops:
  0.0 0.0 copy-start
  0.0 0.0 copy-start.5
  0.1 0.6 copy-done.5
  0.7 0.0 copy-start.4
  0.8 0.7 copy-done.4
  1.4 0.1 constant_dynamic-slice_fusion
  1.5 0.1 copy.79
  1.6 0.1 stack.30
  1.7 0.1 compare_convert_fusion
  1.8 0.0 copy-start.3
  1.9 0.8 copy-done.3
  2.6 0.0 copy-start.1
  2.7 0.9 copy-done.1
  3.5 0.3 fusion.7
  3.8 0.3 fusion.6
  4.1 0.3 fusion.5
  4.4 0.3 fusion.4
  4.7 0.3 fusion.3
  5.1 0.3 fusion.2
  5.4 0.3 fusion.14
  5.7 4.1 %collective-permute-start = (f32[6,16,4]{1,0,2:T(8,128)S(1)}, f32[6,16,4]{1,0,2:T(8,128)S(1)}, u32[]{:S(2)}, u32[]{:S(2)}) collective-permute-start(f32[6,16,4]{1,0,2:T(8,128)S(1)} %get-tuple-element.16), channel_id=1, source_target_pairs={{0,16},{2,18},{4,20},{6,22},{8,24},{10,26},{12,28},{14,30},{16,0},... | collective-permute-start | bytes 4616 | tf_op jit(solution)/shard_map/ppermute | solution.py:13
  9.9 1.3 collective-permute-start.2
  11.1 0.0 collective-permute-start.6
  11.1 0.5 collective-permute-start.7
  11.6 1.5 %collective-permute-start.3 = (f32[6,16,4]{1,0,2:T(8,128)S(1)}, f32[6,16,4]{1,0,2:T(8,128)S(1)}, u32[]{:S(2)}, u32[]{:S(2)}) collective-permute-start(f32[6,16,4]{1,0,2:T(8,128)S(1)} %get-tuple-element.11), channel_id=1, source_target_pairs={{0,2},{2,4},{4,6},{6,8},{8,10},{10,12},{12,14},{14,16},{16,18},{18... | collective-permute-start | bytes 4616 | tf_op jit(solution)/shard_map/ppermute | solution.py:13
  13.1 0.0 collective-permute-done.6
  13.1 2.7 %collective-permute-start.1 = (f32[6,16,4]{1,0,2:T(8,128)S(1)}, f32[6,16,4]{1,0,2:T(8,128)S(1)}, u32[]{:S(2)}, u32[]{:S(2)}) collective-permute-start(f32[6,16,4]{1,0,2:T(8,128)S(1)} %get-tuple-element.15), channel_id=1, source_target_pairs={{0,16},{2,18},{4,20},{6,22},{8,24},{10,26},{12,28},{14,30},{16,0},... | collective-permute-start | bytes 4616 | tf_op jit(solution)/shard_map/ppermute | solution.py:13
  15.8 0.0 collective-permute-done.7
  15.8 2.1 %collective-permute-start.4 = (f32[6,16,4]{1,0,2:T(8,128)S(1)}, f32[6,16,4]{1,0,2:T(8,128)S(1)}, u32[]{:S(2)}, u32[]{:S(2)}) collective-permute-start(f32[6,16,4]{1,0,2:T(8,128)S(1)} %get-tuple-element.14), channel_id=1, source_target_pairs={{0,14},{2,16},{4,18},{6,20},{8,22},{10,24},{12,26},{14,28},{16,30}... | collective-permute-start | bytes 4616 | tf_op jit(solution)/shard_map/ppermute | solution.py:13
  17.9 0.0 collective-permute-done
  17.9 2.8 %collective-permute-start.5 = (f32[6,16,4]{1,0,2:T(8,128)S(1)}, f32[6,16,4]{1,0,2:T(8,128)S(1)}, u32[]{:S(2)}, u32[]{:S(2)}) collective-permute-start(f32[6,16,4]{1,0,2:T(8,128)S(1)} %get-tuple-element.14), channel_id=1, source_target_pairs={{0,30},{2,0},{4,2},{6,4},{8,6},{10,8},{12,10},{14,12},{16,14},{18,... | collective-permute-start | bytes 4616 | tf_op jit(solution)/shard_map/ppermute | solution.py:13
  20.7 0.1 copy.97
  20.8 0.0 copy-start.2
  20.8 0.1 reshape.403
  20.9 0.1 dynamic_slice.11
  21.0 0.0 collective-permute-done.1
  21.0 0.0 collective-permute-done.2
  21.0 0.0 collective-permute-done.3
  21.0 0.3 collective-permute-done.4
  21.3 0.8 collective-permute-done.5
  22.1 0.0 copy-done.2
  22.1 0.3 fusion.13
  22.4 1.8 %all_gather.6 = f32[6,16,8]{1,0,2:T(8,128)S(1)} all-gather(f32[6,16,4]{1,0,2:T(8,128)S(1)} %fusion.13), channel_id=1, replica_groups=mesh['sub'=16,'crs'=2] {'crs'}, dimensions={2}, use_global_device_ids=true | all-gather | bytes 4608 | tf_op jit(solution)/shard_map/all_gather | solution.py:83
  24.3 0.0 copy-done
  24.3 0.2 convolution_bitcast_fusion
  24.5 77.5 %psum.14 = f32[384,16]{0,1:T(8,128)S(1)} all-reduce(f32[384,16]{0,1:T(8,128)S(1)} %convolution_bitcast_fusion), channel_id=1, replica_groups=mesh['sub'=16,'crs'=2] {'sub'}, use_global_device_ids=true, to_apply=%region_1.2 | all-reduce | flops 6144 | bytes 49152 | tf_op jit(solution)/shard_map/psum | solution.py:86
  102.0 0.2 convolution_bitcast_fusion.8
  102.2 0.1 copy.94
  102.3 3.4 %psum.15 = f32[6,16,8]{1,0,2:T(8,128)S(1)} all-reduce(f32[6,16,8]{1,0,2:T(8,128)S(1)} %bitcast.135), channel_id=1, replica_groups=mesh['sub'=16,'crs'=2] {'crs'}, use_global_device_ids=true, to_apply=%region_2.3 | all-reduce | flops 768 | bytes 6144 | tf_op jit(solution)/shard_map/psum | solution.py:92
  105.7 37.6 %all_gather.7 = f32[6,16,128]{1,2,0:T(8,128)S(1)} all-gather(f32[6,16,8]{1,2,0:T(8,128)S(1)} %copy.96), channel_id=1, replica_groups=mesh['sub'=16,'crs'=2] {'sub'}, dimensions={2}, use_global_device_ids=true | all-gather | bytes 52224 | tf_op jit(solution)/shard_map/all_gather | solution.py:94
  143.3 0.3 fusion.44
  143.5 0.1 fusion.74
  143.6 0.4 fusion.35
  144.0 0.4 convolution_add_fusion.5
  144.3 0.4 convolution_add_fusion.4
  144.7 0.4 convolution_add_fusion.3
  145.0 0.4 convolution_add_fusion.2
  145.4 0.4 convolution_add_fusion.1
  145.8 0.4 fusion.1
  146.1 0.7 copy.112
  (22 shorter events, 0.2 us)
Async XLA Ops:
  0.0 24.3 %copy-start = (f32[48,384]{1,0:T(8,128)S(1)}, f32[48,384]{1,0:T(8,128)}, u32[]{:S(2)}) copy-start(f32[48,384]{1,0:T(8,128)} %param.11) | copy-start | bytes 221188
  0.0 0.7 copy-start.5
  0.7 0.7 copy-start.4
  1.8 0.8 copy-start.3
  2.6 0.9 copy-start.1
  5.7 12.2 %collective-permute-start = (f32[6,16,4]{1,0,2:T(8,128)S(1)}, f32[6,16,4]{1,0,2:T(8,128)S(1)}, u32[]{:S(2)}, u32[]{:S(2)}) collective-permute-start(f32[6,16,4]{1,0,2:T(8,128)S(1)} %get-tuple-element.16), channel_id=1, source_target_pairs={{0,16},{2,18},{4,20},{6,22},{8,24},{10,26},{12,28},{14,30},{16,0},... | collective-permute-start | bytes 4616 | tf_op jit(solution)/shard_map/ppermute | solution.py:13
  9.9 11.2 %collective-permute-start.2 = (f32[6,16,4]{1,0,2:T(8,128)S(1)}, f32[6,16,4]{1,0,2:T(8,128)S(1)}, u32[]{:S(2)}, u32[]{:S(2)}) collective-permute-start(f32[6,16,4]{1,0,2:T(8,128)S(1)} %get-tuple-element.11), channel_id=1, source_target_pairs={{0,18},{2,20},{4,22},{6,24},{8,26},{10,28},{12,30},{14,0},{16,2},{... | collective-permute-start | bytes 4616 | tf_op jit(solution)/shard_map/ppermute | solution.py:13
  11.1 2.0 %collective-permute-start.6 = (f32[6,16,1]{1,0,2:T(8,128)S(1)}, f32[6,16,1]{1,0,2:T(8,128)S(1)}, u32[]{:S(2)}, u32[]{:S(2)}) collective-permute-start(f32[6,16,1]{1,0,2:T(8,128)S(1)} %slice.71), channel_id=1, source_target_pairs={{0,1},{1,0},{2,3},{3,2},{4,5},{5,4},{6,7},{7,6},{8,9},{9,8},{10,11... | collective-permute-start | bytes 1160 | tf_op jit(solution)/shard_map/ppermute | solution.py:13
  11.1 4.7 %collective-permute-start.7 = (f32[6,16,1]{1,0,2:T(8,128)S(1)}, f32[6,16,1]{1,0,2:T(8,128)S(1)}, u32[]{:S(2)}, u32[]{:S(2)}) collective-permute-start(f32[6,16,1]{1,0,2:T(8,128)S(1)} %slice.75), channel_id=1, source_target_pairs={{0,1},{1,0},{2,3},{3,2},{4,5},{5,4},{6,7},{7,6},{8,9},{9,8},{10,11... | collective-permute-start | bytes 1160 | tf_op jit(solution)/shard_map/ppermute | solution.py:13
  11.6 9.4 %collective-permute-start.3 = (f32[6,16,4]{1,0,2:T(8,128)S(1)}, f32[6,16,4]{1,0,2:T(8,128)S(1)}, u32[]{:S(2)}, u32[]{:S(2)}) collective-permute-start(f32[6,16,4]{1,0,2:T(8,128)S(1)} %get-tuple-element.11), channel_id=1, source_target_pairs={{0,2},{2,4},{4,6},{6,8},{8,10},{10,12},{12,14},{14,16},{16,18},{18... | collective-permute-start | bytes 4616 | tf_op jit(solution)/shard_map/ppermute | solution.py:13
  13.1 7.9 %collective-permute-start.1 = (f32[6,16,4]{1,0,2:T(8,128)S(1)}, f32[6,16,4]{1,0,2:T(8,128)S(1)}, u32[]{:S(2)}, u32[]{:S(2)}) collective-permute-start(f32[6,16,4]{1,0,2:T(8,128)S(1)} %get-tuple-element.15), channel_id=1, source_target_pairs={{0,16},{2,18},{4,20},{6,22},{8,24},{10,26},{12,28},{14,30},{16,0},... | collective-permute-start | bytes 4616 | tf_op jit(solution)/shard_map/ppermute | solution.py:13
  15.8 5.5 %collective-permute-start.4 = (f32[6,16,4]{1,0,2:T(8,128)S(1)}, f32[6,16,4]{1,0,2:T(8,128)S(1)}, u32[]{:S(2)}, u32[]{:S(2)}) collective-permute-start(f32[6,16,4]{1,0,2:T(8,128)S(1)} %get-tuple-element.14), channel_id=1, source_target_pairs={{0,14},{2,16},{4,18},{6,20},{8,22},{10,24},{12,26},{14,28},{16,30}... | collective-permute-start | bytes 4616 | tf_op jit(solution)/shard_map/ppermute | solution.py:13
  17.9 4.2 %collective-permute-start.5 = (f32[6,16,4]{1,0,2:T(8,128)S(1)}, f32[6,16,4]{1,0,2:T(8,128)S(1)}, u32[]{:S(2)}, u32[]{:S(2)}) collective-permute-start(f32[6,16,4]{1,0,2:T(8,128)S(1)} %get-tuple-element.14), channel_id=1, source_target_pairs={{0,30},{2,0},{4,2},{6,4},{8,6},{10,8},{12,10},{14,12},{16,14},{18,... | collective-permute-start | bytes 4616 | tf_op jit(solution)/shard_map/ppermute | solution.py:13
  20.8 1.3 copy-start.2
where the time goes:
time: 147 us
  blocking collectives  120 us (82%)
  starting transfers between devices  14.9 us (10%)
  matrix products  5.56 us (4%)
  local copies, waits for them, and re-layouts  4.53 us (3%)
    psum x1, blocking collectives, body(): panel_rows = lax.psum(partial_rows, 'sub')  77.5 us
    all_gather x1, blocking collectives, body(): portion = lax.all_gather(group_amps, 'sub', axis=2, tiled=True)  37.6 us
    ppermute x8, starting transfers between devices, shifted(): lax.ppermute(value, axis, [(i, (i + by) % peers) for i in range(peers)])  14.9 us
    psum x1, blocking collectives, body(): group_amps = lax.psum(partial_modes, 'crs')  3.41 us
    unnamed x19, local copies, waits for them, and re-layouts  3.1 us
  transfers between devices with their start and end apart: 8, of which 2 were waited for; matrix products, arithmetic and copies ran while one was open for 0% of the time, Pallas kernels for 0%

commit v1 on v0

--- a/solution.py
+++ b/solution.py
@@ -1,3 +1,4 @@
+import functools
 import jax
 import jax.numpy as jnp
 from jax import lax
@@ -6,6 +7,19 @@
 MODES = 6
 NFACE = 6
 HIGHEST = lax.Precision.HIGHEST
+
+
+def check_points_here(array_in, lane_axis):
+    size_here = lax.axis_size(lane_axis)
+    z2 = array_in
+    for nth in [
+        [(to_i, to_i ^ h) for to_i in range(size_here)] for h in (1, 2, 4, 8, 16) if h < size_here
+    ]:
+        z2 = z2 + lax.ppermute(z2, lane_axis, nth)
+    return z2
+
+
+guide_leaves_for = functools.partial(check_points_here, lane_axis="sub")
 
 
 def shifted(value, axis, by):
@@ -83,7 +97,7 @@
     group_coarse = lax.all_gather(own_total, "crs", axis=2, tiled=True)
     coarse_rhs = group_coarse.transpose(2, 0, 1).reshape(group_subs * MODES, width_rhs)
     partial_rows = jnp.einsum("cp,cr->pr", coarse_factor, coarse_rhs, precision=HIGHEST)
-    panel_rows = lax.psum(partial_rows, "sub")
+    panel_rows = guide_leaves_for(partial_rows)
     partial_modes = jnp.dot(
         coarse_factor, panel_rows, precision=HIGHEST, preferred_element_type=jnp.float32
     )

time: 147 us -> 91.2 us (0.62)
  blocking collectives: 120 us -> 48.1 us
  waiting for transfers between devices: 1.11 us -> 10.5 us
  starting transfers between devices: 14.9 us -> 21.7 us
    psum x1 -> x0, blocking collectives: 77.5 us -> none  [body(): panel_rows = lax.psum(partial_rows, 'sub')]
    ppermute x0 -> x4, waiting for transfers between devices: none -> 8.95 us  [check_points_here(): z2 = z2 + lax.ppermute(z2, lane_axis, nth)]
    ppermute x0 -> x4, starting transfers between devices: none -> 7.42 us  [check_points_here(): z2 = z2 + lax.ppermute(z2, lane_axis, nth)]
    all_gather x1, blocking collectives: 37.6 us -> 42.9 us  [body(): portion = lax.all_gather(group_amps, 'sub', axis=2, tiled=True)]
  transfers between devices with their start and end apart: 8 -> 12, of which waited for: 2 -> 6; matrix products, arithmetic and copies ran while one was open for 0% -> 0% of each run, Pallas kernels for 0% -> 0%
where the time goes in v1:
time: 91.2 us; the launch traced here: 90.9 us
  blocking collectives  48.1 us (53%)
  starting transfers between devices  21.7 us (24%)
  waiting for transfers between devices  10.5 us (12%)
  matrix products  5.57 us (6%)
  local copies, waits for them, and re-layouts  4.52 us (5%)
    all_gather x1, blocking collectives, body(): portion = lax.all_gather(group_amps, 'sub', axis=2, tiled=True)  42.9 us
    ppermute x8, starting transfers between devices, shifted(): lax.ppermute(value, axis, [(i, (i + by) % peers) for i in range(peers)])  14.3 us
    ppermute x4, waiting for transfers between devices, check_points_here(): z2 = z2 + lax.ppermute(z2, lane_axis, nth)  8.95 us
    ppermute x4, starting transfers between devices, check_points_here(): z2 = z2 + lax.ppermute(z2, lane_axis, nth)  7.42 us
    psum x1, blocking collectives, body(): group_amps = lax.psum(partial_modes, 'crs')  3.41 us
    unnamed x19, local copies, waits for them, and re-layouts  3.1 us
    dot_general x6, matrix products, body(): jnp.einsum('ksm,krs->rsm', masked_modes[which_face], near_amps[:, :, :, w...  2.13 us
    all_gather x1, blocking collectives, body(): group_coarse = lax.all_gather(own_total, 'crs', axis=2, tiled=True)  1.83 us
  transfers between devices with their start and end apart: 12, of which 6 were waited for; matrix products, arithmetic and copies ran while one was open for 0% of the time, Pallas kernels for 0%

profile of v1, /device:TPU:0, one launch (start us, length us, event | category | flops | bytes accessed | tf_op | source)
XLA Modules:
  0.0 90.9 jit_solution(18069003466813608449)
XLA Ops:
  0.0 0.0 copy-start
  0.1 0.6 copy-done.5
  0.7 0.0 copy-start.4
  0.8 0.7 copy-done.4
  1.4 0.1 constant_dynamic-slice_fusion
  1.5 0.1 copy.79
  1.6 0.1 stack.30
  1.7 0.1 compare_convert_fusion
  1.8 0.0 copy-start.3
  1.9 0.8 copy-done.3
  2.7 0.9 copy-done.1
  3.5 0.3 fusion.7
  3.8 0.3 fusion.6
  4.1 0.3 fusion.5
  4.4 0.3 fusion.4
  4.7 0.3 fusion.3
  5.1 0.3 fusion.2
  5.4 0.3 fusion.14
  5.7 4.1 %collective-permute-start = (f32[6,16,4]{1,0,2:T(8,128)S(1)}, f32[6,16,4]{1,0,2:T(8,128)S(1)}, u32[]{:S(2)}, u32[]{:S(2)}) collective-permute-start(f32[6,16,4]{1,0,2:T(8,128)S(1)} %get-tuple-element.16), channel_id=1, source_target_pairs={{0,16},{2,18},{4,20},{6,22},{8,24},{10,26},{12,28},{14,30},{16,0},... | collective-permute-start | bytes 4616 | tf_op jit(solution)/shard_map/ppermute | solution.py:27
  9.9 0.0 collective-permute-start.6
  9.9 0.5 collective-permute-start.7
  10.4 1.3 %collective-permute-start.2 = (f32[6,16,4]{1,0,2:T(8,128)S(1)}, f32[6,16,4]{1,0,2:T(8,128)S(1)}, u32[]{:S(2)}, u32[]{:S(2)}) collective-permute-start(f32[6,16,4]{1,0,2:T(8,128)S(1)} %get-tuple-element.11), channel_id=1, source_target_pairs={{0,18},{2,20},{4,22},{6,24},{8,26},{10,28},{12,30},{14,0},{16,2},{... | collective-permute-start | bytes 4616 | tf_op jit(solution)/shard_map/ppermute | solution.py:27
  11.6 1.5 %collective-permute-start.3 = (f32[6,16,4]{1,0,2:T(8,128)S(1)}, f32[6,16,4]{1,0,2:T(8,128)S(1)}, u32[]{:S(2)}, u32[]{:S(2)}) collective-permute-start(f32[6,16,4]{1,0,2:T(8,128)S(1)} %get-tuple-element.11), channel_id=1, source_target_pairs={{0,2},{2,4},{4,6},{6,8},{8,10},{10,12},{12,14},{14,16},{16,18},{18... | collective-permute-start | bytes 4616 | tf_op jit(solution)/shard_map/ppermute | solution.py:27
  13.1 0.0 collective-permute-done.6
  13.1 2.6 %collective-permute-start.1 = (f32[6,16,4]{1,0,2:T(8,128)S(1)}, f32[6,16,4]{1,0,2:T(8,128)S(1)}, u32[]{:S(2)}, u32[]{:S(2)}) collective-permute-start(f32[6,16,4]{1,0,2:T(8,128)S(1)} %get-tuple-element.15), channel_id=1, source_target_pairs={{0,16},{2,18},{4,20},{6,22},{8,24},{10,26},{12,28},{14,30},{16,0},... | collective-permute-start | bytes 4616 | tf_op jit(solution)/shard_map/ppermute | solution.py:27
  15.7 0.0 collective-permute-done.7
  15.7 2.1 %collective-permute-start.4 = (f32[6,16,4]{1,0,2:T(8,128)S(1)}, f32[6,16,4]{1,0,2:T(8,128)S(1)}, u32[]{:S(2)}, u32[]{:S(2)}) collective-permute-start(f32[6,16,4]{1,0,2:T(8,128)S(1)} %get-tuple-element.14), channel_id=1, source_target_pairs={{0,14},{2,16},{4,18},{6,20},{8,22},{10,24},{12,26},{14,28},{16,30}... | collective-permute-start | bytes 4616 | tf_op jit(solution)/shard_map/ppermute | solution.py:27
  17.8 0.0 collective-permute-done
  17.8 2.2 %collective-permute-start.5 = (f32[6,16,4]{1,0,2:T(8,128)S(1)}, f32[6,16,4]{1,0,2:T(8,128)S(1)}, u32[]{:S(2)}, u32[]{:S(2)}) collective-permute-start(f32[6,16,4]{1,0,2:T(8,128)S(1)} %get-tuple-element.14), channel_id=1, source_target_pairs={{0,30},{2,0},{4,2},{6,4},{8,6},{10,8},{12,10},{14,12},{16,14},{18,... | collective-permute-start | bytes 4616 | tf_op jit(solution)/shard_map/ppermute | solution.py:27
  20.0 0.0 collective-permute-done.1
  20.0 0.0 collective-permute-done.2
  20.1 0.0 collective-permute-done.3
  20.1 1.2 %collective-permute-done.4 = f32[6,16,4]{1,0,2:T(8,128)S(1)} collective-permute-done((f32[6,16,4]{1,0,2:T(8,128)S(1)}, f32[6,16,4]{1,0,2:T(8,128)S(1)}, u32[]{:S(2)}, u32[]{:S(2)}) %collective-permute-start.4) | collective-permute-done | bytes 1568 | tf_op jit(solution)/shard_map/ppermute | solution.py:27
  21.3 0.3 collective-permute-done.5
  21.6 0.0 copy-done.2
  21.6 0.3 fusion.13
  21.9 1.8 %all_gather.6 = f32[6,16,8]{1,0,2:T(8,128)S(1)} all-gather(f32[6,16,4]{1,0,2:T(8,128)S(1)} %fusion.13), channel_id=1, replica_groups=mesh['sub'=16,'crs'=2] {'crs'}, dimensions={2}, use_global_device_ids=true | all-gather | bytes 4608 | tf_op jit(solution)/shard_map/all_gather | solution.py:97
  23.7 0.0 copy-done
  23.7 0.2 convolution_bitcast_fusion
  23.9 2.1 %collective-permute-start.8 = (f32[384,16]{0,1:T(8,128)S(1)}, f32[384,16]{0,1:T(8,128)S(1)}, u32[]{:S(2)}, u32[]{:S(2)}) collective-permute-start(f32[384,16]{0,1:T(8,128)S(1)} %convolution_bitcast_fusion), channel_id=1, source_target_pairs={{0,2},{2,0},{4,6},{6,4},{8,10},{10,8},{12,14},{14,12},{16,18},{18,... | collective-permute-start | bytes 73736 | tf_op jit(solution)/shard_map/ppermute | solution.py:18
  26.1 1.8 %collective-permute-done.8 = f32[384,16]{0,1:T(8,128)S(1)} collective-permute-done((f32[384,16]{0,1:T(8,128)S(1)}, f32[384,16]{0,1:T(8,128)S(1)}, u32[]{:S(2)}, u32[]{:S(2)}) %collective-permute-start.8) | collective-permute-done | bytes 24608 | tf_op jit(solution)/shard_map/ppermute | solution.py:18
  27.9 2.4 %collective-permute-start.9 = (f32[384,16]{0,1:T(8,128)S(1)}, f32[384,16]{0,1:T(8,128)S(1)}, u32[]{:S(2)}, u32[]{:S(2)}) collective-permute-start(f32[384,16]{0,1:T(8,128)S(1)} %add.470), channel_id=1, source_target_pairs={{0,4},{2,6},{4,0},{6,2},{8,12},{10,14},{12,8},{14,10},{16,20},{18,... | collective-permute-start | bytes 73736 | tf_op jit(solution)/shard_map/ppermute | solution.py:18
  30.3 1.8 %collective-permute-done.9 = f32[384,16]{0,1:T(8,128)S(1)} collective-permute-done((f32[384,16]{0,1:T(8,128)S(1)}, f32[384,16]{0,1:T(8,128)S(1)}, u32[]{:S(2)}, u32[]{:S(2)}) %collective-permute-start.9) | collective-permute-done | bytes 24608 | tf_op jit(solution)/shard_map/ppermute | solution.py:18
  32.1 1.2 %collective-permute-start.10 = (f32[384,16]{0,1:T(8,128)S(1)}, f32[384,16]{0,1:T(8,128)S(1)}, u32[]{:S(2)}, u32[]{:S(2)}) collective-permute-start(f32[384,16]{0,1:T(8,128)S(1)} %add.471), channel_id=1, source_target_pairs={{0,8},{2,10},{4,12},{6,14},{8,0},{10,2},{12,4},{14,6},{16,24},{18,... | collective-permute-start | bytes 73736 | tf_op jit(solution)/shard_map/ppermute | solution.py:18
  33.3 2.6 %collective-permute-done.10 = f32[384,16]{0,1:T(8,128)S(1)} collective-permute-done((f32[384,16]{0,1:T(8,128)S(1)}, f32[384,16]{0,1:T(8,128)S(1)}, u32[]{:S(2)}, u32[]{:S(2)}) %collective-permute-start.10) | collective-permute-done | bytes 24608 | tf_op jit(solution)/shard_map/ppermute | solution.py:18
  35.9 1.7 %collective-permute-start.11 = (f32[384,16]{0,1:T(8,128)S(1)}, f32[384,16]{0,1:T(8,128)S(1)}, u32[]{:S(2)}, u32[]{:S(2)}) collective-permute-start(f32[384,16]{0,1:T(8,128)S(1)} %add.472), channel_id=1, source_target_pairs={{0,16},{2,18},{4,20},{6,22},{8,24},{10,26},{12,28},{14,30},{16,0},... | collective-permute-start | bytes 73736 | tf_op jit(solution)/shard_map/ppermute | solution.py:18
  37.6 0.1 copy.97
  37.7 0.1 reshape.403
  37.9 0.1 dynamic_slice.11
  38.0 2.7 %collective-permute-done.11 = f32[384,16]{0,1:T(8,128)S(1)} collective-permute-done((f32[384,16]{0,1:T(8,128)S(1)}, f32[384,16]{0,1:T(8,128)S(1)}, u32[]{:S(2)}, u32[]{:S(2)}) %collective-permute-start.11) | collective-permute-done | bytes 24608 | tf_op jit(solution)/shard_map/ppermute | solution.py:18
  40.7 0.2 convolution_bitcast_fusion.8
  40.9 0.1 copy.94
  40.9 3.4 %psum.7 = f32[6,16,8]{1,0,2:T(8,128)S(1)} all-reduce(f32[6,16,8]{1,0,2:T(8,128)S(1)} %bitcast.134), channel_id=1, replica_groups=mesh['sub'=16,'crs'=2] {'crs'}, use_global_device_ids=true, to_apply=%region_1.2 | all-reduce | flops 768 | bytes 6144 | tf_op jit(solution)/shard_map/psum | solution.py:106
  44.4 42.9 %all_gather.7 = f32[6,16,128]{1,2,0:T(8,128)S(1)} all-gather(f32[6,16,8]{1,2,0:T(8,128)S(1)} %copy.96), channel_id=1, replica_groups=mesh['sub'=16,'crs'=2] {'sub'}, dimensions={2}, use_global_device_ids=true | all-gather | bytes 52224 | tf_op jit(solution)/shard_map/all_gather | solution.py:108
  87.3 0.3 fusion.45
  87.5 0.1 fusion.75
  87.6 0.4 fusion.35
  88.0 0.4 convolution_add_fusion.5
  88.3 0.4 convolution_add_fusion.4
  88.7 0.4 convolution_add_fusion.3
  89.1 0.4 convolution_add_fusion.2
  89.4 0.4 convolution_add_fusion.1
  89.8 0.4 fusion.1
  90.1 0.7 copy.112
  (28 shorter events, 0.3 us)
Async XLA Ops:
  0.0 23.7 %copy-start = (f32[48,384]{1,0:T(8,128)S(1)}, f32[48,384]{1,0:T(8,128)}, u32[]{:S(2)}) copy-start(f32[48,384]{1,0:T(8,128)} %param.11) | copy-start | bytes 221188
  0.0 0.7 copy-start.5
  0.7 0.7 copy-start.4
  1.8 0.8 copy-start.3
  2.6 0.9 copy-start.1
  5.7 12.1 %collective-permute-start = (f32[6,16,4]{1,0,2:T(8,128)S(1)}, f32[6,16,4]{1,0,2:T(8,128)S(1)}, u32[]{:S(2)}, u32[]{:S(2)}) collective-permute-start(f32[6,16,4]{1,0,2:T(8,128)S(1)} %get-tuple-element.16), channel_id=1, source_target_pairs={{0,16},{2,18},{4,20},{6,22},{8,24},{10,26},{12,28},{14,30},{16,0},... | collective-permute-start | bytes 4616 | tf_op jit(solution)/shard_map/ppermute | solution.py:27
  9.9 11.7 %copy-start.2 = (f32[6,4,512]{2,1,0:T(4,128)S(1)}, f32[6,4,512]{2,1,0:T(4,128)}, u32[]{:S(2)}) copy-start(f32[6,4,512]{2,1,0:T(4,128)} %param.7) | copy-start | bytes 147460
  9.9 3.3 %collective-permute-start.6 = (f32[6,16,1]{1,0,2:T(8,128)S(1)}, f32[6,16,1]{1,0,2:T(8,128)S(1)}, u32[]{:S(2)}, u32[]{:S(2)}) collective-permute-start(f32[6,16,1]{1,0,2:T(8,128)S(1)} %slice.71), channel_id=1, source_target_pairs={{0,1},{1,0},{2,3},{3,2},{4,5},{5,4},{6,7},{7,6},{8,9},{9,8},{10,11... | collective-permute-start | bytes 1160 | tf_op jit(solution)/shard_map/ppermute | solution.py:27
  9.9 5.9 %collective-permute-start.7 = (f32[6,16,1]{1,0,2:T(8,128)S(1)}, f32[6,16,1]{1,0,2:T(8,128)S(1)}, u32[]{:S(2)}, u32[]{:S(2)}) collective-permute-start(f32[6,16,1]{1,0,2:T(8,128)S(1)} %slice.75), channel_id=1, source_target_pairs={{0,1},{1,0},{2,3},{3,2},{4,5},{5,4},{6,7},{7,6},{8,9},{9,8},{10,11... | collective-permute-start | bytes 1160 | tf_op jit(solution)/shard_map/ppermute | solution.py:27
  10.4 9.7 %collective-permute-start.2 = (f32[6,16,4]{1,0,2:T(8,128)S(1)}, f32[6,16,4]{1,0,2:T(8,128)S(1)}, u32[]{:S(2)}, u32[]{:S(2)}) collective-permute-start(f32[6,16,4]{1,0,2:T(8,128)S(1)} %get-tuple-element.11), channel_id=1, source_target_pairs={{0,18},{2,20},{4,22},{6,24},{8,26},{10,28},{12,30},{14,0},{16,2},{... | collective-permute-start | bytes 4616 | tf_op jit(solution)/shard_map/ppermute | solution.py:27
  11.6 8.4 %collective-permute-start.3 = (f32[6,16,4]{1,0,2:T(8,128)S(1)}, f32[6,16,4]{1,0,2:T(8,128)S(1)}, u32[]{:S(2)}, u32[]{:S(2)}) collective-permute-start(f32[6,16,4]{1,0,2:T(8,128)S(1)} %get-tuple-element.11), channel_id=1, source_target_pairs={{0,2},{2,4},{4,6},{6,8},{8,10},{10,12},{12,14},{14,16},{16,18},{18... | collective-permute-start | bytes 4616 | tf_op jit(solution)/shard_map/ppermute | solution.py:27
  13.1 6.9 %collective-permute-start.1 = (f32[6,16,4]{1,0,2:T(8,128)S(1)}, f32[6,16,4]{1,0,2:T(8,128)S(1)}, u32[]{:S(2)}, u32[]{:S(2)}) collective-permute-start(f32[6,16,4]{1,0,2:T(8,128)S(1)} %get-tuple-element.15), channel_id=1, source_target_pairs={{0,16},{2,18},{4,20},{6,22},{8,24},{10,26},{12,28},{14,30},{16,0},... | collective-permute-start | bytes 4616 | tf_op jit(solution)/shard_map/ppermute | solution.py:27
  15.7 5.5 %collective-permute-start.4 = (f32[6,16,4]{1,0,2:T(8,128)S(1)}, f32[6,16,4]{1,0,2:T(8,128)S(1)}, u32[]{:S(2)}, u32[]{:S(2)}) collective-permute-start(f32[6,16,4]{1,0,2:T(8,128)S(1)} %get-tuple-element.14), channel_id=1, source_target_pairs={{0,14},{2,16},{4,18},{6,20},{8,22},{10,24},{12,26},{14,28},{16,30}... | collective-permute-start | bytes 4616 | tf_op jit(solution)/shard_map/ppermute | solution.py:27
  17.8 3.7 %collective-permute-start.5 = (f32[6,16,4]{1,0,2:T(8,128)S(1)}, f32[6,16,4]{1,0,2:T(8,128)S(1)}, u32[]{:S(2)}, u32[]{:S(2)}) collective-permute-start(f32[6,16,4]{1,0,2:T(8,128)S(1)} %get-tuple-element.14), channel_id=1, source_target_pairs={{0,30},{2,0},{4,2},{6,4},{8,6},{10,8},{12,10},{14,12},{16,14},{18,... | collective-permute-start | bytes 4616 | tf_op jit(solution)/shard_map/ppermute | solution.py:27
  23.9 3.9 %collective-permute-start.8 = (f32[384,16]{0,1:T(8,128)S(1)}, f32[384,16]{0,1:T(8,128)S(1)}, u32[]{:S(2)}, u32[]{:S(2)}) collective-permute-start(f32[384,16]{0,1:T(8,128)S(1)} %convolution_bitcast_fusion), channel_id=1, source_target_pairs={{0,2},{2,0},{4,6},{6,4},{8,10},{10,8},{12,14},{14,12},{16,18},{18,... | collective-permute-start | bytes 73736 | tf_op jit(solution)/shard_map/ppermute | solution.py:18
  27.9 4.2 %collective-permute-start.9 = (f32[384,16]{0,1:T(8,128)S(1)}, f32[384,16]{0,1:T(8,128)S(1)}, u32[]{:S(2)}, u32[]{:S(2)}) collective-permute-start(f32[384,16]{0,1:T(8,128)S(1)} %add.470), channel_id=1, source_target_pairs={{0,4},{2,6},{4,0},{6,2},{8,12},{10,14},{12,8},{14,10},{16,20},{18,... | collective-permute-start | bytes 73736 | tf_op jit(solution)/shard_map/ppermute | solution.py:18
  32.1 3.8 %collective-permute-start.10 = (f32[384,16]{0,1:T(8,128)S(1)}, f32[384,16]{0,1:T(8,128)S(1)}, u32[]{:S(2)}, u32[]{:S(2)}) collective-permute-start(f32[384,16]{0,1:T(8,128)S(1)} %add.471), channel_id=1, source_target_pairs={{0,8},{2,10},{4,12},{6,14},{8,0},{10,2},{12,4},{14,6},{16,24},{18,... | collective-permute-start | bytes 73736 | tf_op jit(solution)/shard_map/ppermute | solution.py:18
  35.9 4.7 %collective-permute-start.11 = (f32[384,16]{0,1:T(8,128)S(1)}, f32[384,16]{0,1:T(8,128)S(1)}, u32[]{:S(2)}, u32[]{:S(2)}) collective-permute-start(f32[384,16]{0,1:T(8,128)S(1)} %add.472), channel_id=1, source_target_pairs={{0,16},{2,18},{4,20},{6,22},{8,24},{10,26},{12,28},{14,30},{16,0},... | collective-permute-start | bytes 73736 | tf_op jit(solution)/shard_map/ppermute | solution.py:18
